TPU v7x, 32 devices: a whole 2x2x4 slice. The times are simulated.
32 devices in a mesh: gx: 4 (over x, core), gy: 8 (over z, y).
Axes of the slice: x: 2, y: 2, z: 4, core: 2. Of those that a mesh axis runs over, the one named last changes fastest.
Arguments:
- table: bfloat16 [32768, 512], P('gy'), may hold values from -40 to 40
- history: bfloat16 [2, 32, 1024, 512], P(None, 'gy', 'gx'), may hold values from -40 to 40
- lengths: int32 [8, 4], P('gy'), may hold values from 341 to 1024, as said below
- assignment: int32 [8, 4], P('gy'), may hold values from 0 to 3, each once within a row
- cand_owner: int32 [49152, 1], P(('gx', 'gy')), may hold values from 0 to 7; in each aligned block of 1536 rows (0 to 1535, 1536 to 3071, ...) at most 384 rows name the same one
- cand_row: int32 [49152], P(('gx', 'gy')), may hold values from 0 to 4095
- norm_gain: float32 [2, 512], replicated, may hold values from 0.1 to 1.9
- w_query: bfloat16 [2, 512, 1024], replicated, may hold values from -0.5 to 0.5
- w_key: bfloat16 [2, 512, 1024], replicated, may hold values from -1 to 1
- attn_gain: float32 [2, 512], replicated, may hold values from 0.1 to 1.9
- w_out: bfloat16 [2, 512, 512], replicated, may hold values from -0.25 to 0.25
Outputs:
- cand_out: bfloat16 [49152, 512], P(('gx', 'gy'))
Inputs may be any that keep to these rules, and one draw needn't show every extreme that they name: `lengths`: some user has exactly 1024 live positions and some exactly 341. `assignment`: each row names each of its column's 4 users once. `cand_owner`: within the 1536 candidates of one device no table shard is named more than 384 times.
All inputs are finite; a program needn't handle non-finite values.
Results may differ from a plain program's by a relative error of at most 0.0075.
Values may be sent and summed in bfloat16 or wider, within the bound.
No kernel may reach another device: no remote copies, remote signals or barrier semaphores. Data moves between devices by JAX's collectives and lax.ppermute only.
A program may use at most 128 MiB of HBM per device.

v0:
```python
import functools

import jax
import jax.numpy as jnp
from jax import lax
from jax.experimental import pallas as pl
from jax.experimental.pallas import tpu as pltpu
from jax.sharding import PartitionSpec as P


HEADS = 4
EPSILON = 1e-06
NT = (((1,), (1,)), ((), ()))
KEY_TILE = 256
LANES = 128
F32, BF16 = jnp.float32, jnp.bfloat16


def half_silu(half):
    return half + half * jnp.tanh(half)


def rms_scale(vector, gain_row):
    scale = lax.rsqrt(jnp.mean(vector * vector, axis=-1, keepdims=True) + EPSILON)
    return vector * scale * gain_row


def params(mib, *semantics):
    return pltpu.CompilerParams(
        dimension_semantics=semantics or None, vmem_limit_bytes=mib * 2**20
    )


def cost(flops, moved):
    return pl.CostEstimate(flops=int(flops), bytes_accessed=int(moved), transcendentals=0)


def iota(shape, axis):
    return lax.broadcasted_iota(jnp.int32, shape, axis).astype(F32)


def column(row):
    return jnp.broadcast_to(row, (8, row.shape[1])).T[:, 0:1]


def requests_kernel(
    rows,
    members,
    fast_cap,
    first_cap,
    first_count,
    owner_ref,
    row_ref,
    assignment_ref,
    history_ref,
    req_ref,
    rank_ref,
    *refs,
):
    sent, (held, read_sems, write_sems) = refs[: members - 1], refs[members - 1 :]
    own = lax.axis_index("gx")
    reads, writes = [], []
    for shift, out in enumerate(sent, 1):
        user = assignment_ref[0, lax.rem(own + shift, members)]
        block = held.at[shift - 1]
        reads.append(
            pltpu.make_async_copy(history_ref.at[:, user], block, read_sems.at[shift - 1])
        )
        writes.append(pltpu.make_async_copy(block, out, write_sems.at[shift - 1]))
    for copy in reads:
        copy.start()
    groups = req_ref.shape[0]
    capacity = req_ref.shape[2] - LANES
    count = owner_ref.shape[1]
    owner = owner_ref[...].astype(F32)
    row = row_ref[...].astype(F32)
    key = owner * rows + row
    keys = column(key)
    place = iota((1, count), 1)
    step = 128
    first = jnp.full((8, count), float(count), F32)
    for base in range(0, count, step):
        same = keys[base : base + step] == key
        at = jnp.where(same, iota((step, 1), 0) + base, float(count))
        first = jnp.minimum(first, jnp.min(at.reshape(step // 8, 8, count), axis=0))
    first = jnp.min(first, axis=0, keepdims=True)
    for read, write in zip(reads, writes):
        read.wait()
        write.start()
    owned = iota((groups, 1), 0) == owner
    leads = jnp.where(owned & (first == place), 1.0, 0.0)
    prior = jnp.zeros((groups, count), F32)
    step = 256
    for base in range(0, count, step):
        before = jnp.where(iota((step, 1), 0) + base < first, 1.0, 0.0).astype(BF16)
        prior += jnp.dot(
            leads[:, base : base + step].astype(BF16), before, preferred_element_type=F32
        )
    rank = jnp.sum(jnp.where(owned, prior, 0.0), axis=0, keepdims=True)
    high = jnp.floor(row * (1.0 / 256))
    low = row - high * 256
    parts = jnp.concatenate([leads * high, leads * low], axis=0).astype(BF16)
    at_slot = jnp.where(iota((capacity, 1), 0) == rank, 1.0, 0.0).astype(BF16)
    listed = lax.dot_general(parts, at_slot, NT, preferred_element_type=F32)
    asked = listed[:groups] * 256 + listed[groups:]
    most = jnp.max(jnp.sum(leads, axis=1, keepdims=True), axis=0, keepdims=True)
    ready = jnp.sum(jnp.where(rank < first_cap, 1.0, 0.0), axis=1, keepdims=True)
    slow = (most > fast_cap) | (ready < first_count)
    flag = jnp.broadcast_to(jnp.where(slow, 1, 0).astype(jnp.int32), (1, LANES))
    asked = asked.astype(jnp.int32)
    for g in range(groups):
        req_ref[g, :, :capacity] = asked[g : g + 1]
        req_ref[g, :, capacity:] = flag
    rank_ref[...] = rank.astype(jnp.int32)
    for write in writes:
        write.wait()


def order_kernel(groups, fast_cap, first_cap, owner_ref, rank_ref, pos_ref, slot_ref):
    count = owner_ref.shape[1]
    owner = owner_ref[...].astype(F32)
    rank = rank_ref[...].astype(F32)
    key = rank * count + iota((1, count), 1)
    keys = column(key)
    step = 128
    smaller = jnp.zeros((8, count), F32)
    for base in range(0, count, step):
        less = jnp.where(keys[base : base + step] < key, 1.0, 0.0)
        smaller += jnp.sum(less.reshape(step // 8, 8, count), axis=0)
    pos = jnp.sum(smaller, axis=0, keepdims=True)
    pos_ref[...] = column(pos)
    rest = fast_cap - first_cap
    slot = jnp.where(
        rank < first_cap,
        owner * first_cap + rank,
        groups * first_cap + owner * rest + (rank - first_cap),
    )
    for base in range(0, count, step):
        here = jnp.where(iota((step, 1), 0) + base == pos, slot, 0.0)
        slot_ref[base : base + step, :] = jnp.sum(here, axis=1, keepdims=True)


def lookup_kernel(offset, ids_ref, table_ref, _, out_ref, select):
    groups, length, features = out_ref.shape
    lanes = iota((1, table_ref.shape[0]), 1)
    for g in range(groups):
        ids = column(ids_ref[g].astype(F32))[offset : offset + length]
        hit = jnp.where(ids == lanes, 1.0, 0.0)
        select[g * length : (g + 1) * length, :] = hit.astype(BF16)
    found = jnp.dot(select[...], table_ref[...], preferred_element_type=F32)
    out_ref[...] = found.astype(BF16).reshape(groups, length, features)


def lookup(ids, table, after, offset, length):
    groups = ids.shape[0]
    rows, features = table.shape
    whole = lambda a: pl.BlockSpec(a.shape, lambda i: (0,) * a.ndim)
    return pl.pallas_call(
        functools.partial(lookup_kernel, offset),
        grid=(1,),
        in_specs=[whole(ids), whole(table), pl.BlockSpec(after.shape if after.shape[0] < 8 else (8, after.shape[1]), lambda i: (0, 0))],
        out_specs=pl.BlockSpec((groups, length, features), lambda i: (0, 0, 0)),
        out_shape=jax.ShapeDtypeStruct((groups, length, features), BF16),
        scratch_shapes=[pltpu.VMEM((groups * length, rows), BF16)],
        compiler_params=params(30, "arbitrary"),
        cost_estimate=cost(2 * groups * length * rows * features, table.size * 2),
        name="lookup",
    )(ids, table, after)


def pick_kernel(base, count, added, slot_ref, *refs):
    out_ref = refs[-1]
    slot = slot_ref[...]
    total = None
    for ref in refs[:count]:
        size = ref.shape[0]
        hit = jnp.where(slot == iota((1, size), 1) + base, 1.0, 0.0).astype(BF16)
        found = jnp.dot(hit, ref[...], preferred_element_type=F32)
        total = found if total is None else total + found
        base += size
    if added:
        total = total + refs[count][...].astype(F32)
    out_ref[...] = total.astype(out_ref.dtype)


def pick(slots, sources, base, first, amount, tile, addend=None, after=None):
    features = sources[0].shape[1]
    lead = first // tile
    size = sum(source.shape[0] for source in sources)
    row_block = pl.BlockSpec((tile, features), lambda i: (i, 0))
    return pl.pallas_call(
        functools.partial(pick_kernel, base, len(sources), addend is not None),
        grid=(amount // tile,),
        in_specs=[pl.BlockSpec((tile, 1), lambda i: (i + lead, 0))]
        + [pl.BlockSpec(source.shape, lambda i: (0, 0)) for source in sources]
        + ([] if addend is None else [row_block])
        + ([] if after is None else [pl.BlockSpec((16, features), lambda i: (0, 0))]),
        out_specs=row_block,
        out_shape=jax.ShapeDtypeStruct((amount, features), BF16),
        compiler_params=params(16, "arbitrary"),
        cost_estimate=cost(2 * amount * size * features, size * features * 2),
        name="pick",
    )(slots, *sources, *[x for x in (addend, after) if x is not None])


def project_kernel(members, assignment_ref, lengths_ref, history_ref, *refs):
    blocks = refs[: members - 1]
    gain_ref, weight_ref, key_ref, value_ref, own_block, sem = refs[members - 1 :]
    span, features = own_block.shape
    layer = pl.program_id(0)
    own = lax.axis_index("gx")
    user = assignment_ref[0, own]
    length = lengths_ref[0, user]
    copy = pltpu.make_async_copy(history_ref.at[layer, user], own_block, sem)
    copy.start()
    copy.wait()
    for shift in range(members):
        states = own_block[...] if shift == 0 else blocks[shift - 1][0]
        normed = rms_scale(states.astype(F32), gain_ref[0]).astype(BF16)
        half = 0.5 * jnp.dot(normed, weight_ref[0], preferred_element_type=F32)
        key_value = half_silu(half)
        start = pl.multiple_of(lax.rem(own - shift + members, members) * span, span)
        live = lax.broadcasted_iota(jnp.int32, (span, 1), 0) + start < length
        key_ref[0, pl.ds(start, span), :] = key_value[:, :features].astype(BF16)
        value = jnp.where(live, key_value[:, features:], 0.0)
        value_ref[0, pl.ds(start, span), :] = value.astype(BF16)


def project(assignment, lengths, history, blocks, gain, weight):
    layers, _, span, features = history.shape
    members = len(blocks) + 1
    per_layer = lambda *shape: pl.BlockSpec((1,) + shape, lambda i: (i, 0, 0))
    whole = jax.ShapeDtypeStruct((layers, span * members, features), BF16)
    return pl.pallas_call(
        functools.partial(project_kernel, members),
        grid=(layers,),
        in_specs=[
            pl.BlockSpec(memory_space=pltpu.SMEM),
            pl.BlockSpec(memory_space=pltpu.SMEM),
            pl.BlockSpec(memory_space=pltpu.HBM),
        ]
        + [per_layer(span, features)] * (members - 1)
        + [per_layer(1, features), per_layer(features, 2 * features)],
        out_specs=[per_layer(span * members, features)] * 2,
        out_shape=[whole] * 2,
        scratch_shapes=[pltpu.VMEM((span, features), BF16), pltpu.SemaphoreType.DMA],
        compiler_params=params(20, "arbitrary"),
        cost_estimate=cost(4 * layers * span * members * features**2, history.size * 4),
        name="project",
    )(assignment, lengths, history, *blocks, gain.reshape(layers, 1, features), weight)


def layers_kernel(x_ref, key_ref, value_ref, ng_ref, wq_ref, ag_ref, wo_ref, out_ref):
    layers, total, features = key_ref.shape
    size = features // HEADS
    scale = 0.5 * size**-0.5
    x = x_ref[...].astype(F32)
    for layer in range(layers):
        normed = rms_scale(x, ng_ref[layer : layer + 1, :]).astype(BF16)
        weight = wq_ref[layer]
        gate = jnp.dot(normed, weight[:, :features], preferred_element_type=F32)
        gate = half_silu(0.5 * gate).astype(BF16)
        query = jnp.dot(normed, weight[:, features:], preferred_element_type=F32)
        query = (half_silu(0.5 * query) * scale).astype(BF16)
        heads = []
        for head in range(HEADS):
            columns = slice(head * size, (head + 1) * size)
            attended = None
            for base in range(0, total, KEY_TILE):
                rows = slice(base, base + KEY_TILE)
                half = lax.dot_general(
                    query[:, columns],
                    key_ref[layer, rows, columns],
                    NT,
                    preferred_element_type=F32,
                )
                part = jnp.dot(
                    half_silu(half).astype(BF16),
                    value_ref[layer, rows, columns],
                    preferred_element_type=F32,
                )
                attended = part if attended is None else attended + part
            heads.append(attended)
        attended = rms_scale(jnp.concatenate(heads, axis=1), ag_ref[layer : layer + 1, :])
        gated = (attended * gate.astype(F32)).astype(BF16)
        x = x + jnp.dot(gated, wo_ref[layer], preferred_element_type=F32)
    out_ref[...] = x.astype(BF16)


def run_layers(x, tile, keys, values, norm_gain, w_query, attn_gain, w_out):
    amount, features = x.shape
    layers, total, _ = keys.shape
    full = lambda a: pl.BlockSpec(a.shape, lambda i: (0,) * a.ndim)
    shared = (keys, values, norm_gain, w_query, attn_gain, w_out)
    flops = layers * amount * features * (6 * features + 8 * total)
    return pl.pallas_call(
        layers_kernel,
        grid=(amount // tile,),
        in_specs=[pl.BlockSpec((tile, features), lambda i: (i, 0))] + [full(a) for a in shared],
        out_specs=pl.BlockSpec((tile, features), lambda i: (i, 0)),
        out_shape=jax.ShapeDtypeStruct((amount, features), BF16),
        compiler_params=params(32, "arbitrary"),
        cost_estimate=cost(flops, keys.size * 8),
        name="run_layers",
    )(x, *shared)


def local(
    table,
    history,
    lengths,
    assignment,
    cand_owner,
    cand_row,
    norm_gain,
    w_query,
    w_key,
    attn_gain,
    w_out,
):
    groups = lax.axis_size("gy")
    members = lax.axis_size("gx")
    count = cand_row.shape[0]
    rows, features = table.shape
    capacity = 2 * count // groups
    fast_cap = 5 * capacity // 8
    first_cap = capacity // 3
    tile = count // 4
    first_count = 3 * tile

    layers, _, span, _ = history.shape
    owner = cand_owner.reshape(1, count)
    row = cand_row.reshape(1, count)
    block = jax.ShapeDtypeStruct((layers, span, features), BF16)
    others = members - 1
    vmem, smem = pl.BlockSpec(memory_space=pltpu.VMEM), pl.BlockSpec(memory_space=pltpu.SMEM)
    hbm = pl.BlockSpec(memory_space=pltpu.HBM)
    requests, rank, *sent = pl.pallas_call(
        functools.partial(requests_kernel, rows, members, fast_cap, first_cap, first_count),
        in_specs=[vmem, vmem, smem, hbm],
        out_specs=[vmem, vmem] + [hbm] * others,
        out_shape=[
            jax.ShapeDtypeStruct((groups, 1, capacity + LANES), jnp.int32),
            jax.ShapeDtypeStruct((1, count), jnp.int32),
        ]
        + [block] * others,
        scratch_shapes=[
            pltpu.VMEM((others, layers, span, features), BF16),
            pltpu.SemaphoreType.DMA((others,)),
            pltpu.SemaphoreType.DMA((others,)),
        ],
        compiler_params=params(16),
        cost_estimate=cost(8 * count * count, 1),
        name="requests",
    )(owner, row, assignment, history)

    def exchange(block):
        return lax.all_to_all(block, "gy", split_axis=0, concat_axis=0, tiled=True)

    ids = exchange(requests)
    blocks = [
        lax.ppermute(block, "gx", [(j, (j + shift) % members) for j in range(members)])
        for shift, block in enumerate(sent, 1)
    ]
    slow = jnp.any(ids[:, 0, capacity] > 0)
    pos, slots = pl.pallas_call(
        functools.partial(order_kernel, groups, fast_cap, first_cap),
        out_shape=[jax.ShapeDtypeStruct((count, 1), F32)] * 2,
        compiler_params=params(12),
        cost_estimate=cost(8 * count * count, 1),
        name="order",
    )(owner, rank)

    second_cap = fast_cap - first_cap
    found_1 = lookup(ids, table, norm_gain, 0, first_cap)
    arrived_1 = exchange(found_1)
    found_2 = lookup(ids, table, slots, first_cap, second_cap)
    arrived_2 = exchange(found_2)
    arrived_1 = arrived_1.reshape(groups * first_cap, features)
    arrived_2 = arrived_2.reshape(groups * second_cap, features)
    keys, values = project(assignment, lengths, history, blocks, norm_gain, w_key)
    shared = (keys, values, norm_gain, w_query, attn_gain, w_out)
    early = run_layers(pick(slots, (arrived_1,), 0, 0, first_count, tile), tile, *shared)
    placed = pick(pos, (early,), 0, 0, count, tile)
    late = pick(
        slots, (arrived_1, arrived_2), 0, first_count, count - first_count, tile, after=placed
    )
    late = run_layers(late, tile, *shared)

    def in_order(operands):
        pos, placed, late = operands
        return pick(pos, (late,), first_count, 0, count, tile, placed)

    def in_full(operands):
        arrived = exchange(jnp.take(table, ids[:, 0, :capacity], axis=0, mode="clip"))
        place = (owner * capacity + rank).reshape(count)
        embedded = jnp.take(arrived.reshape(groups * capacity, features), place, axis=0, mode="clip")
        return run_layers(embedded, tile, *shared)

    return lax.cond(slow, in_full, in_order, (pos, placed, late))


def solution(mesh):
    return jax.shard_map(
        local,
        mesh=mesh,
        in_specs=(
            P("gy", None),
            P(None, "gy", "gx", None),
            P("gy", None),
            P("gy", None),
            P(("gx", "gy"), None),
            P(("gx", "gy")),
            P(),
            P(),
            P(),
            P(),
            P(),
        ),
        out_specs=P(("gx", "gy"), None),
        check_vma=False,
    )
```

profile of v0, /device:TPU:0, one launch (start us, length us, event | category | flops | bytes accessed | tf_op | source)
XLA Modules:
  0.0 106.4 jit_solution(10702752038838352447)
XLA Ops:
  0.0 0.7 reshape.24.row_ref
  0.7 1.6 %copy-done = bf16[2,4,256,512]{3,2,1,0:T(8,128)(2,1)S(1)} copy-done((bf16[2,4,256,512]{3,2,1,0:T(8,128)(2,1)S(1)}, bf16[2,4,256,512]{3,2,1,0:T(8,128)(2,1)}, u32[]{:S(2)}) %copy-start) | copy-done | bytes 2097176
  2.3 0.7 copy-done.2
  3.0 3.4 %requests.1 = (s32[8,1,512]{2,1,0:T(1,128)S(1)}, s32[1,1536]{1,0:T(1,128)S(1)}, bf16[2,256,512]{2,1,0:T(8,128)(2,1)}, bf16[2,256,512]{2,1,0:T(8,128)(2,1)}, bf16[2,256,512]{2,1,0:T(8,128)(2,1)S(1)}) custom-call(s32[1,1536]{1,0:T(1,128)} %bitcast.11, s32[1,1536]{1,0:T(1,128)S(1)} %reshape.24.row_ref, s32[1,4]{1,0:T(1,128)S(1)} %copy-done.2, ...), custom_call_target="tpu_custom_call" | custom-call | flops 18874368 | bytes 1 | tf_op jit(solution)/shard_map/requests/pallas_call | solution.py:338
  6.4 13.7 %all_to_all.19.ids_ref = s32[8,1,512]{2,1,0:T(1,128)S(1)} all-to-all(s32[8,1,512]{2,1,0:T(1,128)S(1)} %get-tuple-element.56), channel_id=1, replica_groups=mesh['gx'=4,'gy'=8] {'gy'}, dimensions={0} | all-to-all | bytes 32768 | tf_op jit(solution)/shard_map/all_to_all | solution.py:358
  20.0 0.0 copy-done.10
  20.0 8.1 %lookup.2 = bf16[8,128,512]{2,1,0:T(8,128)(2,1)} custom-call(s32[8,1,512]{2,1,0:T(1,128)S(1)} %all_to_all.19.ids_ref, bf16[4096,512]{1,0:T(8,128)(2,1)} %table_ref.3, f32[2,512]{1,0:T(2,128)S(1)} %copy-done.10), custom_call_target="tpu_custom_call" | custom-call | flops 4294967296 | bytes 4194304 | tf_op jit(solution)/shard_map/lookup/pallas_call | solution.py:158
  28.1 3.7 %all-to-all-start.2 = ((bf16[8,128,512]{2,1,0:T(8,128)(2,1)}), bf16[8,128,512]{2,1,0:T(8,128)(2,1)S(1)}, u32[]{:S(2)}, u32[]{:S(2)}) async-start(bf16[8,128,512]{2,1,0:T(8,128)(2,1)} %lookup.2), calls=%async_computation.2 | async-start | bytes 2097152 | tf_op jit(solution)/shard_map/all_to_all | solution.py:358
  31.8 0.1 collective-permute-start
  31.9 1.6 %collective-permute-start.1 = (bf16[2,256,512]{2,1,0:T(8,128)(2,1)}, bf16[2,256,512]{2,1,0:T(8,128)(2,1)}, u32[]{:S(2)}, u32[]{:S(2)}) collective-permute-start(bf16[2,256,512]{2,1,0:T(8,128)(2,1)} %get-tuple-element.61), channel_id=1, source_target_pairs={{0,16},{8,24},{16,0},{24,8},{1,17},{9,25},{17,1},{25,9},{2,18},{10... | collective-permute-start | bytes 1572872 | tf_op jit(solution)/shard_map/ppermute | solution.py:362
  33.4 1.4 %collective-permute-start.2 = (bf16[2,256,512]{2,1,0:T(8,128)(2,1)S(1)}, bf16[2,256,512]{2,1,0:T(8,128)(2,1)}, u32[]{:S(2)}, u32[]{:S(2)}) collective-permute-start(bf16[2,256,512]{2,1,0:T(8,128)(2,1)S(1)} %get-tuple-element.62), channel_id=1, source_target_pairs={{0,24},{8,0},{16,8},{24,16},{1,25},{9,1},{17,9},{25,17},{2,26},{10... | collective-permute-start | bytes 1572872 | tf_op jit(solution)/shard_map/ppermute | solution.py:362
  34.8 0.0 copy-done.9
  34.8 2.5 %order.1 = (f32[1536,1]{1,0:T(8,128)}, f32[1536,1]{1,0:T(8,128)S(1)}) custom-call(s32[1,1536]{1,0:T(1,128)S(1)} %bitcast.12, s32[1,1536]{1,0:T(1,128)S(1)} %get-tuple-element.57.rank_ref), custom_call_target="tpu_custom_call" | custom-call | flops 18874368 | bytes 1 | tf_op jit(solution)/shard_map/order/pallas_call | solution.py:366
  37.3 0.7 compare_reduce_fusion
  38.6 0.0 copy-start.3
  38.6 0.0 copy-start.5
  38.6 7.4 %lookup.3 = bf16[8,112,512]{2,1,0:T(8,128)(2,1)} custom-call(s32[8,1,512]{2,1,0:T(1,128)S(1)} %all_to_all.19.ids_ref, bf16[4096,512]{1,0:T(8,128)(2,1)} %table_ref.3, f32[1536,1]{1,0:T(8,128)S(1)} %get-tuple-element.59._.slot_ref), custom_call_target="tpu_custom_call" | custom-call | flops 3758096384 | bytes 4194304 | tf_op jit(solution)/shard_map/lookup/pallas_call | solution.py:158
  46.0 10.5 %all-to-all-done.2 = bf16[8,128,512]{2,1,0:T(8,128)(2,1)S(1)} async-done(((bf16[8,128,512]{2,1,0:T(8,128)(2,1)}), bf16[8,128,512]{2,1,0:T(8,128)(2,1)S(1)}, u32[]{:S(2)}, u32[]{:S(2)}) %all-to-all-start.2) | async-done | bytes 1048608 | tf_op jit(solution)/shard_map/all_to_all | solution.py:358
  56.5 3.7 %all-to-all-start.3 = ((bf16[8,112,512]{2,1,0:T(8,128)(2,1)}), bf16[8,112,512]{2,1,0:T(8,128)(2,1)S(1)}, u32[]{:S(2)}, u32[]{:S(2)}) async-start(bf16[8,112,512]{2,1,0:T(8,128)(2,1)} %lookup.3), calls=%async_computation.3 | async-start | bytes 1835008 | tf_op jit(solution)/shard_map/all_to_all | solution.py:358
  60.3 0.0 collective-permute-done.refs_0_
  60.3 0.0 collective-permute-done.1.refs_1_
  60.3 0.0 collective-permute-done.2.refs_2_
  60.3 0.0 copy-done.3
  60.3 0.0 copy-done.5
  60.3 0.0 copy-start.1
  60.3 1.6 %copy-done.1 = bf16[2,4,256,512]{3,2,1,0:T(8,128)(2,1)S(1)} copy-done((bf16[2,4,256,512]{3,2,1,0:T(8,128)(2,1)S(1)}, bf16[2,4,256,512]{3,2,1,0:T(8,128)(2,1)}, u32[]{:S(2)}) %copy-start.1) | copy-done | bytes 2097176
  61.9 1.6 %copy-done.4 = bf16[2,512,1024]{2,1,0:T(8,128)(2,1)S(1)} copy-done((bf16[2,512,1024]{2,1,0:T(8,128)(2,1)S(1)}, bf16[2,512,1024]{2,1,0:T(8,128)(2,1)}, u32[]{:S(2)}) %copy-start.4) | copy-done | bytes 2097176
  63.5 5.1 %project.1 = (bf16[2,1024,512]{2,1,0:T(8,128)(2,1)S(1)}, bf16[2,1024,512]{2,1,0:T(8,128)(2,1)S(1)}) custom-call(s32[1,4]{1,0:T(1,128)S(1)} %copy-done.3, s32[1,4]{1,0:T(1,128)S(1)} %copy-done.5, bf16[2,4,256,512]{3,2,1,0:T(8,128)(2,1)S(1)} %copy-done.1, bf16[2,256,512]{2,1,0:T(8,128)(2,1)} %collective-permute-done.refs_0_, ...), custom_call_target="tpu_custom_call" | custom-call | flops 2147483648 | bytes 4194304 | tf_op jit(solution)/shard_map/project/pallas_call | solution.py:234
  68.6 0.0 copy-start.19
  68.6 0.0 copy-start.20
  68.6 0.0 copy-start.11
  68.6 0.0 copy-start.14
  68.6 0.0 copy-start.18
  68.6 1.9 %pick.5.x_ref = bf16[1152,512]{1,0:T(8,128)(2,1)S(1)} custom-call(f32[1536,1]{1,0:T(8,128)S(1)} %get-tuple-element.59._.slot_ref, bf16[1024,512]{1,0:T(8,128)(2,1)S(1)} %bitcast.6), custom_call_target="tpu_custom_call" | custom-call | flops 1207959552 | bytes 1048576 | tf_op jit(solution)/shard_map/pick/pallas_call | solution.py:191
  70.6 0.0 copy-done.19
  70.6 0.1 copy-done.20
  70.7 1.0 copy-done.11
  71.7 0.3 copy-done.14
  72.0 0.0 copy-done.18
  72.0 17.7 %run_layers.4.refs_0_ = bf16[1152,512]{1,0:T(8,128)(2,1)S(1)} custom-call(bf16[1152,512]{1,0:T(8,128)(2,1)S(1)} %pick.5.x_ref, bf16[2,1024,512]{2,1,0:T(8,128)(2,1)S(1)} %get-tuple-element.63.key_ref, bf16[2,1024,512]{2,1,0:T(8,128)(2,1)S(1)} %get-tuple-element.64.value_ref, f32[2,512]{1,0:T(2,128)S(1)} %copy-done.10, bf16[2,512,1024]{2,1,0:T(8,128)(2,1)S(1)} %copy-done.11, ...), custom_call_target="tpu_custom_call" | custom-call | flops 13287555072 | bytes 8388608 | tf_op jit(solution)/shard_map/run_layers/pallas_call | solution.py:296
  89.7 0.0 copy-done.7
  89.7 3.7 %pick.6.refs_2_ = bf16[1536,512]{1,0:T(8,128)(2,1)} custom-call(f32[1536,1]{1,0:T(8,128)S(1)} %copy-done.7, bf16[1152,512]{1,0:T(8,128)(2,1)S(1)} %run_layers.4.refs_0_), custom_call_target="tpu_custom_call" | custom-call | flops 1811939328 | bytes 1179648 | tf_op jit(solution)/shard_map/pick/pallas_call | solution.py:191
  93.4 0.0 all-to-all-done.3
  93.4 1.9 %pick.7.x_ref = bf16[384,512]{1,0:T(8,128)(2,1)S(1)} custom-call(f32[1536,1]{1,0:T(8,128)S(1)} %get-tuple-element.59._.slot_ref, bf16[1024,512]{1,0:T(8,128)(2,1)S(1)} %bitcast.7, bf16[896,512]{1,0:T(8,128)(2,1)S(1)} %bitcast.8, bf16[1536,512]{1,0:T(8,128)(2,1)} %pick.6.refs_2_), custom_call_target="tpu_custom_call" | custom-call | flops 754974720 | bytes 1966080 | tf_op jit(solution)/shard_map/pick/pallas_call | solution.py:191
  95.3 0.0 copy-start.6
  95.3 8.2 %run_layers.5 = bf16[384,512]{1,0:T(8,128)(2,1)S(1)} custom-call(bf16[384,512]{1,0:T(8,128)(2,1)S(1)} %pick.7.x_ref, bf16[2,1024,512]{2,1,0:T(8,128)(2,1)} %copy-done.19, bf16[2,1024,512]{2,1,0:T(8,128)(2,1)} %copy-done.20, f32[2,512]{1,0:T(2,128)S(1)} %copy-done.10, bf16[2,512,1024]{2,1,0:T(8,128)(2,1)S(1)} %copy-done.12, f32[2,512]{1,0:T(2,128)S(1)} %copy-done.18, ...), custom_call_target="tpu_custom_call" | custom-call | flops 4429185024 | bytes 8388608 | tf_op jit(solution)/shard_map/run_layers/pallas_call | solution.py:296
  103.6 2.8 %conditional.1 = (bf16[1536,512]{1,0:T(8,128)(2,1)}) conditional(s32[]{:T(128)} %convert_element_type.3, (f32[1536,1]{1,0:T(8,128)S(1)}, bf16[384,512]{1,0:T(8,128)(2,1)S(1)}, bf16[1536,512]{1,0:T(8,128)(2,1)S(1)}) %tuple.18, (s32[8,1,512]{2,1,0:T(1,128)S(1)}, bf16[4096,512]{1,0:T(8,128)(2,1)}, s32[1,1536]{1,0:T(1,128)S(1)}, s32[1,1536]{1,0:T(1,128)S(1)}, ...), branch_computations={%region_1.0_spmd, %region_2.3_spmd} | conditional | flops 17716748288 | bytes 44140668 | solution.py:400
  103.6 2.8 %pick.4 = bf16[1536,512]{1,0:T(8,128)(2,1)} custom-call(f32[1536,1]{1,0:T(8,128)S(1)} %get-tuple-element.34.slot_ref, bf16[384,512]{1,0:T(8,128)(2,1)S(1)} %get-tuple-element.35.refs_0_, bf16[1536,512]{1,0:T(8,128)(2,1)S(1)} %get-tuple-element.36.refs_1_), custom_call_target="tpu_custom_call" | custom-call | flops 603979776 | bytes 393216 | tf_op jit(solution)/shard_map/cond/branch_0_fun/pick/pallas_call | solution.py:191
  (14 shorter events, 0.0 us)
Async XLA Ops:
  0.0 20.0 %copy-start.10 = (f32[2,512]{1,0:T(2,128)S(1)}, f32[2,512]{1,0:T(2,128)}, u32[]{:S(2)}) copy-start(f32[2,512]{1,0:T(2,128)} %ng_ref.3) | copy-start | bytes 12292
  0.7 1.6 %copy-start = (bf16[2,4,256,512]{3,2,1,0:T(8,128)(2,1)S(1)}, bf16[2,4,256,512]{3,2,1,0:T(8,128)(2,1)}, u32[]{:S(2)}) copy-start(bf16[2,4,256,512]{3,2,1,0:T(8,128)(2,1)} %history_ref.3) | copy-start | bytes 6291460
  2.3 0.7 copy-start.2
  28.1 6.7 %copy-start.9 = (s32[1536,1]{0,1:T(1,128)S(1)}, s32[1536,1]{0,1:T(1,128)}, u32[]{:S(2)}) copy-start(s32[1536,1]{0,1:T(1,128)} %param.17) | copy-start | bytes 18436
  28.1 28.4 %all-to-all-start.2 = ((bf16[8,128,512]{2,1,0:T(8,128)(2,1)}), bf16[8,128,512]{2,1,0:T(8,128)(2,1)S(1)}, u32[]{:S(2)}, u32[]{:S(2)}) async-start(bf16[8,128,512]{2,1,0:T(8,128)(2,1)} %lookup.2), calls=%async_computation.2 | async-start | bytes 2097152 | tf_op jit(solution)/shard_map/all_to_all | solution.py:358
  31.8 28.5 %collective-permute-start = (bf16[2,256,512]{2,1,0:T(8,128)(2,1)}, bf16[2,256,512]{2,1,0:T(8,128)(2,1)}, u32[]{:S(2)}, u32[]{:S(2)}) collective-permute-start(bf16[2,256,512]{2,1,0:T(8,128)(2,1)} %get-tuple-element.60), channel_id=1, source_target_pairs={{0,8},{8,16},{16,24},{24,0},{1,9},{9,17},{17,25},{25,1},{2,10},{10... | collective-permute-start | bytes 1572872 | tf_op jit(solution)/shard_map/ppermute | solution.py:362
  31.9 28.4 %collective-permute-start.1 = (bf16[2,256,512]{2,1,0:T(8,128)(2,1)}, bf16[2,256,512]{2,1,0:T(8,128)(2,1)}, u32[]{:S(2)}, u32[]{:S(2)}) collective-permute-start(bf16[2,256,512]{2,1,0:T(8,128)(2,1)} %get-tuple-element.61), channel_id=1, source_target_pairs={{0,16},{8,24},{16,0},{24,8},{1,17},{9,25},{17,1},{25,9},{2,18},{10... | collective-permute-start | bytes 1572872 | tf_op jit(solution)/shard_map/ppermute | solution.py:362
  33.4 26.9 %collective-permute-start.2 = (bf16[2,256,512]{2,1,0:T(8,128)(2,1)S(1)}, bf16[2,256,512]{2,1,0:T(8,128)(2,1)}, u32[]{:S(2)}, u32[]{:S(2)}) collective-permute-start(bf16[2,256,512]{2,1,0:T(8,128)(2,1)S(1)} %get-tuple-element.62), channel_id=1, source_target_pairs={{0,24},{8,0},{16,8},{24,16},{1,25},{9,1},{17,9},{25,17},{2,26},{10... | collective-permute-start | bytes 1572872 | tf_op jit(solution)/shard_map/ppermute | solution.py:362
  38.6 21.7 %copy-start.3 = (s32[1,4]{1,0:T(1,128)S(1)}, s32[1,4]{1,0:T(1,128)}, u32[]{:S(2)}) copy-start(s32[1,4]{1,0:T(1,128)} %assignment_ref.3) | copy-start | bytes 52
  38.6 21.7 %copy-start.5 = (s32[1,4]{1,0:T(1,128)S(1)}, s32[1,4]{1,0:T(1,128)}, u32[]{:S(2)}) copy-start(s32[1,4]{1,0:T(1,128)} %lengths_ref.1) | copy-start | bytes 52
  56.5 36.9 %all-to-all-start.3 = ((bf16[8,112,512]{2,1,0:T(8,128)(2,1)}), bf16[8,112,512]{2,1,0:T(8,128)(2,1)S(1)}, u32[]{:S(2)}, u32[]{:S(2)}) async-start(bf16[8,112,512]{2,1,0:T(8,128)(2,1)} %lookup.3), calls=%async_computation.3 | async-start | bytes 1835008 | tf_op jit(solution)/shard_map/all_to_all | solution.py:358
  60.3 1.6 %copy-start.1 = (bf16[2,4,256,512]{3,2,1,0:T(8,128)(2,1)S(1)}, bf16[2,4,256,512]{3,2,1,0:T(8,128)(2,1)}, u32[]{:S(2)}) copy-start(bf16[2,4,256,512]{3,2,1,0:T(8,128)(2,1)} %history_ref.3) | copy-start | bytes 6291460
  61.9 1.6 %copy-start.4 = (bf16[2,512,1024]{2,1,0:T(8,128)(2,1)S(1)}, bf16[2,512,1024]{2,1,0:T(8,128)(2,1)}, u32[]{:S(2)}) copy-start(bf16[2,512,1024]{2,1,0:T(8,128)(2,1)} %refs_4_.1) | copy-start | bytes 6291460
  68.6 2.0 %copy-start.19 = (bf16[2,1024,512]{2,1,0:T(8,128)(2,1)}, bf16[2,1024,512]{2,1,0:T(8,128)(2,1)S(1)}, u32[]{:S(2)}) copy-start(bf16[2,1024,512]{2,1,0:T(8,128)(2,1)S(1)} %get-tuple-element.63.key_ref) | copy-start | bytes 6291460
  68.6 2.1 %copy-start.20 = (bf16[2,1024,512]{2,1,0:T(8,128)(2,1)}, bf16[2,1024,512]{2,1,0:T(8,128)(2,1)S(1)}, u32[]{:S(2)}) copy-start(bf16[2,1024,512]{2,1,0:T(8,128)(2,1)S(1)} %get-tuple-element.64.value_ref) | copy-start | bytes 6291460
  68.6 3.1 %copy-start.11 = (bf16[2,512,1024]{2,1,0:T(8,128)(2,1)S(1)}, bf16[2,512,1024]{2,1,0:T(8,128)(2,1)}, u32[]{:S(2)}) copy-start(bf16[2,512,1024]{2,1,0:T(8,128)(2,1)} %wq_ref.3) | copy-start | bytes 6291460
  68.6 3.4 %copy-start.14 = (bf16[2,512,512]{2,1,0:T(8,128)(2,1)S(1)}, bf16[2,512,512]{2,1,0:T(8,128)(2,1)}, u32[]{:S(2)}) copy-start(bf16[2,512,512]{2,1,0:T(8,128)(2,1)} %wo_ref.3) | copy-start | bytes 3145732
  68.6 3.3 %copy-start.18 = (f32[2,512]{1,0:T(2,128)S(1)}, f32[2,512]{1,0:T(2,128)}, u32[]{:S(2)}) copy-start(f32[2,512]{1,0:T(2,128)} %ag_ref.3) | copy-start | bytes 12292
  72.0 17.8 %copy-start.7 = (f32[1536,1]{1,0:T(8,128)S(1)}, f32[1536,1]{1,0:T(8,128)}, u32[]{:S(2)}) copy-start(f32[1536,1]{1,0:T(8,128)} %get-tuple-element.58.slot_ref) | copy-start | bytes 18436
  93.4 1.9 %copy-start.12 = (bf16[2,512,1024]{2,1,0:T(8,128)(2,1)S(1)}, bf16[2,512,1024]{2,1,0:T(8,128)(2,1)}, u32[]{:S(2)}) copy-start(bf16[2,512,1024]{2,1,0:T(8,128)(2,1)} %wq_ref.3) | copy-start | bytes 6291460
  93.4 1.9 %copy-start.15 = (bf16[2,512,512]{2,1,0:T(8,128)(2,1)S(1)}, bf16[2,512,512]{2,1,0:T(8,128)(2,1)}, u32[]{:S(2)}) copy-start(bf16[2,512,512]{2,1,0:T(8,128)(2,1)} %wo_ref.3) | copy-start | bytes 3145732
  95.3 8.3 %copy-start.6 = (bf16[1536,512]{1,0:T(8,128)(2,1)S(1)}, bf16[1536,512]{1,0:T(8,128)(2,1)}, u32[]{:S(2)}) copy-start(bf16[1536,512]{1,0:T(8,128)(2,1)} %pick.6.refs_2_) | copy-start | bytes 4718596
  95.3 8.3 %copy-start.8 = (f32[1536,1]{1,0:T(8,128)S(1)}, f32[1536,1]{1,0:T(8,128)}, u32[]{:S(2)}) copy-start(f32[1536,1]{1,0:T(8,128)} %get-tuple-element.58.slot_ref) | copy-start | bytes 18436
where the time goes:
time: 107 us; the launch traced here: 106 us
  Pallas kernels  62.6 us (59%)
  blocking collectives  13.7 us (13%)
  waiting for transfers between devices  10.5 us (10%)
  starting transfers between devices  10.4 us (10%)
  local copies, waits for them, and re-layouts  7.59 us (7%)
    pallas_call x2, Pallas kernels, run_layers(): pl.pallas_call(layers_kernel, grid=(amount // tile,), in_specs=[pl.BlockS...  26 us
    pallas_call x2, Pallas kernels, lookup(): pl.pallas_call(functools.partial(lookup_kernel, offset), grid=(1,), in_sp...  15.5 us
    all_to_all x1, blocking collectives, exchange(): return lax.all_to_all(block, 'gy', split_axis=0, concat_axis=0, tiled=True)  13.7 us
    all_to_all x2, waiting for transfers between devices, exchange(): return lax.all_to_all(block, 'gy', split_axis=0, concat_axis=0, tiled=True)  10.5 us
    pallas_call x4, Pallas kernels, pick(): pl.pallas_call(functools.partial(pick_kernel, base, len(sources), addend...  10.2 us
    all_to_all x2, starting transfers between devices, exchange(): return lax.all_to_all(block, 'gy', split_axis=0, concat_axis=0, tiled=True)  7.42 us
    unnamed x36, local copies, waits for them, and re-layouts  6.87 us
    pallas_call x1, Pallas kernels, project(): pl.pallas_call(functools.partial(project_kernel, members), grid=(layers,)...  5.06 us
  transfers between devices with their start and end apart: 5, of which 1 were waited for; matrix products, arithmetic and copies ran while one was open for 1% of the time, Pallas kernels for 36%

commit v1 on v0

--- a/solution.py
+++ b/solution.py
@@ -73,7 +73,7 @@
     capacity = req_ref.shape[2] - LANES
     count = owner_ref.shape[1]
     owner = owner_ref[...].astype(F32)
-    row = row_ref[...].astype(F32)
+    row = row_ref[...].reshape(1, count).astype(F32)
     key = owner * rows + row
     keys = column(key)
     place = iota((1, count), 1)
@@ -140,13 +140,16 @@
         slot_ref[base : base + step, :] = jnp.sum(here, axis=1, keepdims=True)
 
 
-def lookup_kernel(offset, ids_ref, table_ref, _, out_ref, select):
+def lookup_kernel(offset, ids_ref, source_ref, _, out_ref, select, table_ref, sem):
+    copy = pltpu.make_async_copy(source_ref, table_ref, sem)
+    copy.start()
     groups, length, features = out_ref.shape
     lanes = iota((1, table_ref.shape[0]), 1)
     for g in range(groups):
         ids = column(ids_ref[g].astype(F32))[offset : offset + length]
         hit = jnp.where(ids == lanes, 1.0, 0.0)
         select[g * length : (g + 1) * length, :] = hit.astype(BF16)
+    copy.wait()
     found = jnp.dot(select[...], table_ref[...], preferred_element_type=F32)
     out_ref[...] = found.astype(BF16).reshape(groups, length, features)
 
@@ -154,53 +157,65 @@
 def lookup(ids, table, after, offset, length):
     groups = ids.shape[0]
     rows, features = table.shape
-    whole = lambda a: pl.BlockSpec(a.shape, lambda i: (0,) * a.ndim)
+    part = (min(8, after.shape[0]), after.shape[1])
     return pl.pallas_call(
         functools.partial(lookup_kernel, offset),
         grid=(1,),
-        in_specs=[whole(ids), whole(table), pl.BlockSpec(after.shape if after.shape[0] < 8 else (8, after.shape[1]), lambda i: (0, 0))],
+        in_specs=[
+            pl.BlockSpec(ids.shape, lambda i: (0, 0, 0)),
+            pl.BlockSpec(memory_space=pltpu.HBM),
+            pl.BlockSpec(part, lambda i: (0, 0)),
+        ],
         out_specs=pl.BlockSpec((groups, length, features), lambda i: (0, 0, 0)),
         out_shape=jax.ShapeDtypeStruct((groups, length, features), BF16),
-        scratch_shapes=[pltpu.VMEM((groups * length, rows), BF16)],
-        compiler_params=params(30, "arbitrary"),
+        scratch_shapes=[
+            pltpu.VMEM((groups * length, rows), BF16),
+            pltpu.VMEM((rows, features), BF16),
+            pltpu.SemaphoreType.DMA,
+        ],
+        compiler_params=params(44, "arbitrary"),
         cost_estimate=cost(2 * groups * length * rows * features, table.size * 2),
         name="lookup",
     )(ids, table, after)
 
 
-def pick_kernel(base, count, added, slot_ref, *refs):
-    out_ref = refs[-1]
-    slot = slot_ref[...]
+def picked(slot, refs, base):
     total = None
-    for ref in refs[:count]:
+    for ref in refs:
         size = ref.shape[0]
         hit = jnp.where(slot == iota((1, size), 1) + base, 1.0, 0.0).astype(BF16)
         found = jnp.dot(hit, ref[...], preferred_element_type=F32)
         total = found if total is None else total + found
         base += size
-    if added:
-        total = total + refs[count][...].astype(F32)
+    return total
+
+
+def pick_kernel(base, slot_ref, source_ref, *refs):
+    out_ref = refs[-1]
+    total = picked(slot_ref[...], (source_ref,), base)
+    for ref in refs[:-1]:
+        total = total + ref[...].astype(F32)
     out_ref[...] = total.astype(out_ref.dtype)
 
 
-def pick(slots, sources, base, first, amount, tile, addend=None, after=None):
-    features = sources[0].shape[1]
-    lead = first // tile
-    size = sum(source.shape[0] for source in sources)
+def pick(slots, source, base, tile, *addends):
+    amount = slots.shape[0]
+    size, features = source.shape
     row_block = pl.BlockSpec((tile, features), lambda i: (i, 0))
     return pl.pallas_call(
-        functools.partial(pick_kernel, base, len(sources), addend is not None),
+        functools.partial(pick_kernel, base),
         grid=(amount // tile,),
-        in_specs=[pl.BlockSpec((tile, 1), lambda i: (i + lead, 0))]
-        + [pl.BlockSpec(source.shape, lambda i: (0, 0)) for source in sources]
-        + ([] if addend is None else [row_block])
-        + ([] if after is None else [pl.BlockSpec((16, features), lambda i: (0, 0))]),
+        in_specs=[
+            pl.BlockSpec((tile, 1), lambda i: (i, 0)),
+            pl.BlockSpec(source.shape, lambda i: (0, 0)),
+        ]
+        + [row_block] * len(addends),
         out_specs=row_block,
         out_shape=jax.ShapeDtypeStruct((amount, features), BF16),
         compiler_params=params(16, "arbitrary"),
         cost_estimate=cost(2 * amount * size * features, size * features * 2),
         name="pick",
-    )(slots, *sources, *[x for x in (addend, after) if x is not None])
+    )(slots, source, *addends)
 
 
 def project_kernel(members, assignment_ref, lengths_ref, history_ref, *refs):
@@ -250,11 +265,29 @@
     )(assignment, lengths, history, *blocks, gain.reshape(layers, 1, features), weight)
 
 
-def layers_kernel(x_ref, key_ref, value_ref, ng_ref, wq_ref, ag_ref, wo_ref, out_ref):
+def layers_kernel(count, slot_ref, *refs):
+    sources, refs = refs[:count], refs[count:]
+    keys_ref, values_ref, ng_ref, wq_ref, ag_ref, wo_ref = refs[:6]
+    out_ref, key_ref, value_ref, sems = refs[-4:]
     layers, total, features = key_ref.shape
+    opening = pl.program_id(0) == 0
+    copies = [
+        (
+            pltpu.make_async_copy(keys_ref.at[layer], key_ref.at[layer], sems.at[2 * layer]),
+            pltpu.make_async_copy(values_ref.at[layer], value_ref.at[layer], sems.at[2 * layer + 1]),
+        )
+        for layer in range(layers)
+    ]
+
+    @pl.when(opening)
+    def _():
+        for pair in copies:
+            for copy in pair:
+                copy.start()
+
     size = features // HEADS
     scale = 0.5 * size**-0.5
-    x = x_ref[...].astype(F32)
+    x = picked(slot_ref[...], sources, 0)
     for layer in range(layers):
         normed = rms_scale(x, ng_ref[layer : layer + 1, :]).astype(BF16)
         weight = wq_ref[layer]
@@ -262,6 +295,12 @@
         gate = half_silu(0.5 * gate).astype(BF16)
         query = jnp.dot(normed, weight[:, features:], preferred_element_type=F32)
         query = (half_silu(0.5 * query) * scale).astype(BF16)
+
+        @pl.when(opening)
+        def _():
+            for copy in copies[layer]:
+                copy.wait()
+
         heads = []
         for head in range(HEADS):
             columns = slice(head * size, (head + 1) * size)
@@ -287,22 +326,28 @@
     out_ref[...] = x.astype(BF16)
 
 
-def run_layers(x, tile, keys, values, norm_gain, w_query, attn_gain, w_out):
-    amount, features = x.shape
-    layers, total, _ = keys.shape
+def run_layers(slots, first, amount, sources, tile, shared, after=()):
+    keys, _, _, _, _, _ = shared
+    layers, total, features = keys.shape
+    lead = first // tile
     full = lambda a: pl.BlockSpec(a.shape, lambda i: (0,) * a.ndim)
-    shared = (keys, values, norm_gain, w_query, attn_gain, w_out)
+    held = pltpu.VMEM(keys.shape, BF16)
     flops = layers * amount * features * (6 * features + 8 * total)
     return pl.pallas_call(
-        layers_kernel,
+        functools.partial(layers_kernel, len(sources)),
         grid=(amount // tile,),
-        in_specs=[pl.BlockSpec((tile, features), lambda i: (i, 0))] + [full(a) for a in shared],
+        in_specs=[pl.BlockSpec((tile, 1), lambda i: (i + lead, 0))]
+        + [full(a) for a in sources]
+        + [pl.BlockSpec(memory_space=pltpu.HBM)] * 2
+        + [full(a) for a in shared[2:]]
+        + [pl.BlockSpec((16, features), lambda i: (0, 0))] * len(after),
         out_specs=pl.BlockSpec((tile, features), lambda i: (i, 0)),
         out_shape=jax.ShapeDtypeStruct((amount, features), BF16),
-        compiler_params=params(32, "arbitrary"),
+        scratch_shapes=[held, held, pltpu.SemaphoreType.DMA((2 * layers,))],
+        compiler_params=params(40, "arbitrary"),
         cost_estimate=cost(flops, keys.size * 8),
         name="run_layers",
-    )(x, *shared)
+    )(slots, *sources, *shared, *after)
 
 
 def local(
@@ -324,13 +369,12 @@
     rows, features = table.shape
     capacity = 2 * count // groups
     fast_cap = 5 * capacity // 8
-    first_cap = capacity // 3
+    first_cap = 7 * capacity // 24
     tile = count // 4
     first_count = 3 * tile
 
     layers, _, span, _ = history.shape
     owner = cand_owner.reshape(1, count)
-    row = cand_row.reshape(1, count)
     block = jax.ShapeDtypeStruct((layers, span, features), BF16)
     others = members - 1
     vmem, smem = pl.BlockSpec(memory_space=pltpu.VMEM), pl.BlockSpec(memory_space=pltpu.SMEM)
@@ -349,10 +393,10 @@
             pltpu.SemaphoreType.DMA((others,)),
             pltpu.SemaphoreType.DMA((others,)),
         ],
-        compiler_params=params(16),
+        compiler_params=params(60),
         cost_estimate=cost(8 * count * count, 1),
         name="requests",
-    )(owner, row, assignment, history)
+    )(owner, cand_row, assignment, history)
 
     def exchange(block):
         return lax.all_to_all(block, "gy", split_axis=0, concat_axis=0, tiled=True)
@@ -380,22 +424,23 @@
     arrived_2 = arrived_2.reshape(groups * second_cap, features)
     keys, values = project(assignment, lengths, history, blocks, norm_gain, w_key)
     shared = (keys, values, norm_gain, w_query, attn_gain, w_out)
-    early = run_layers(pick(slots, (arrived_1,), 0, 0, first_count, tile), tile, *shared)
-    placed = pick(pos, (early,), 0, 0, count, tile)
-    late = pick(
-        slots, (arrived_1, arrived_2), 0, first_count, count - first_count, tile, after=placed
+    early = run_layers(slots, 0, first_count, (arrived_1,), tile, shared)
+    placed = pick(pos, early, 0, tile)
+    late_count = count - first_count
+    late = run_layers(
+        slots, first_count, late_count, (arrived_1, arrived_2), tile, shared, (placed,)
     )
-    late = run_layers(late, tile, *shared)
 
     def in_order(operands):
         pos, placed, late = operands
-        return pick(pos, (late,), first_count, 0, count, tile, placed)
+        return pick(pos, late, first_count, tile, placed)
 
     def in_full(operands):
         arrived = exchange(jnp.take(table, ids[:, 0, :capacity], axis=0, mode="clip"))
         place = (owner * capacity + rank).reshape(count)
         embedded = jnp.take(arrived.reshape(groups * capacity, features), place, axis=0, mode="clip")
-        return run_layers(embedded, tile, *shared)
+        every = jnp.arange(count, dtype=F32).reshape(count, 1)
+        return run_layers(every, 0, count, (embedded,), tile // 4, shared)
 
     return lax.cond(slow, in_full, in_order, (pos, placed, late))
 

time: 107 us -> 101 us (0.944)
  local copies, waits for them, and re-layouts: 7.59 us -> 4.5 us
  waiting for transfers between devices: 10.5 us -> 7.65 us
    all_to_all x2, waiting for transfers between devices: 10.5 us -> 7.65 us  [exchange(): return lax.all_to_all(block, 'gy', split_axis=0, concat_axis=0, tiled=True)]
    unnamed x36 -> x44, local copies, waits for them, and re-layouts: 6.87 us -> 4.49 us
    pallas_call x2, Pallas kernels: 15.5 us -> 13.9 us  [lookup(): pl.pallas_call(functools.partial(lookup_kernel, offset), grid=(1,), in_sp...]
    pallas_call x6 -> x4, Pallas kernels: 36.2 us -> 37.1 us  [the longest x2 30.6 us: run_layers(): pl.pallas_call(functools.partial(layers_kernel, len(sources)), grid=(amou...]
  transfers between devices with their start and end apart: 5 -> 5, of which waited for: 1 -> 1; matrix products, arithmetic and copies ran while one was open for 1% -> 1% of each run, Pallas kernels for 36% -> 39%
where the time goes in v1:
time: 101 us
  Pallas kernels  62.6 us (62%)
  blocking collectives  13.9 us (14%)
  starting transfers between devices  10.3 us (10%)
  waiting for transfers between devices  7.65 us (8%)
  local copies, waits for them, and re-layouts  4.5 us (4%)
    pallas_call x2, Pallas kernels, run_layers(): pl.pallas_call(functools.partial(layers_kernel, len(sources)), grid=(amou...  30.6 us
    pallas_call x2, Pallas kernels, lookup(): pl.pallas_call(functools.partial(lookup_kernel, offset), grid=(1,), in_sp...  13.9 us
    all_to_all x1, blocking collectives, exchange(): return lax.all_to_all(block, 'gy', split_axis=0, concat_axis=0, tiled=True)  13.9 us
    all_to_all x2, waiting for transfers between devices, exchange(): return lax.all_to_all(block, 'gy', split_axis=0, concat_axis=0, tiled=True)  7.65 us
    all_to_all x2, starting transfers between devices, exchange(): return lax.all_to_all(block, 'gy', split_axis=0, concat_axis=0, tiled=True)  7.3 us
    pallas_call x2, Pallas kernels, pick(): pl.pallas_call(functools.partial(pick_kernel, base), grid=(amount // tile...  6.44 us
    pallas_call x1, Pallas kernels, project(): pl.pallas_call(functools.partial(project_kernel, members), grid=(layers,)...  5.06 us
    unnamed x44, local copies, waits for them, and re-layouts  4.49 us
  transfers between devices with their start and end apart: 5, of which 1 were waited for; matrix products, arithmetic and copies ran while one was open for 1% of the time, Pallas kernels for 39%

profile of v1, /device:TPU:0, one launch (start us, length us, event | category | flops | bytes accessed | tf_op | source)
XLA Modules:
  0.0 100.6 jit_solution(5226037628792592478)
XLA Ops:
  0.0 4.0 %requests.1 = (s32[8,1,512]{2,1,0:T(1,128)}, s32[1,1536]{1,0:T(1,128)S(1)}, bf16[2,256,512]{2,1,0:T(8,128)(2,1)}, bf16[2,256,512]{2,1,0:T(8,128)(2,1)}, bf16[2,256,512]{2,1,0:T(8,128)(2,1)}) custom-call(s32[1,1536]{1,0:T(1,128)} %bitcast.12, s32[1536]{0:T(1024)} %row_ref.1, s32[1,4]{1,0:T(1,128)} %assignment_ref.3, bf16[2,4,256,512]{3,2,1,0:T(8,128)(2,1)} %history_ref.3), custom_call_target="tpu_custom_call" | custom-call | flops 18874368 | bytes 1 | tf_op jit(solution)/shard_map/requests/pallas_call | solution.py:382
  4.0 0.0 copy-start.16
  4.0 13.9 %all_to_all.19.ids_ref = s32[8,1,512]{2,1,0:T(1,128)S(1)} all-to-all(s32[8,1,512]{2,1,0:T(1,128)} %get-tuple-element.56), channel_id=1, replica_groups=mesh['gx'=4,'gy'=8] {'gy'}, dimensions={0} | all-to-all | bytes 32768 | tf_op jit(solution)/shard_map/all_to_all | solution.py:402
  17.9 0.0 copy-done.18
  17.9 7.1 %lookup.2 = bf16[8,112,512]{2,1,0:T(8,128)(2,1)} custom-call(s32[8,1,512]{2,1,0:T(1,128)S(1)} %all_to_all.19.ids_ref, bf16[4096,512]{1,0:T(8,128)(2,1)} %source_ref.3, f32[2,512]{1,0:T(2,128)S(1)} %copy-done.18), custom_call_target="tpu_custom_call" | custom-call | flops 3758096384 | bytes 4194304 | tf_op jit(solution)/shard_map/lookup/pallas_call | solution.py:161
  25.0 3.6 %all-to-all-start.2 = ((bf16[8,112,512]{2,1,0:T(8,128)(2,1)}), bf16[8,112,512]{2,1,0:T(8,128)(2,1)S(1)}, u32[]{:S(2)}, u32[]{:S(2)}) async-start(bf16[8,112,512]{2,1,0:T(8,128)(2,1)} %lookup.2), calls=%async_computation.2 | async-start | bytes 1835008 | tf_op jit(solution)/shard_map/all_to_all | solution.py:402
  28.6 0.1 collective-permute-start
  28.6 1.6 %collective-permute-start.1 = (bf16[2,256,512]{2,1,0:T(8,128)(2,1)}, bf16[2,256,512]{2,1,0:T(8,128)(2,1)}, u32[]{:S(2)}, u32[]{:S(2)}) collective-permute-start(bf16[2,256,512]{2,1,0:T(8,128)(2,1)} %get-tuple-element.61), channel_id=1, source_target_pairs={{0,16},{8,24},{16,0},{24,8},{1,17},{9,25},{17,1},{25,9},{2,18},{10... | collective-permute-start | bytes 1572872 | tf_op jit(solution)/shard_map/ppermute | solution.py:406
  30.2 1.4 %collective-permute-start.2 = (bf16[2,256,512]{2,1,0:T(8,128)(2,1)}, bf16[2,256,512]{2,1,0:T(8,128)(2,1)}, u32[]{:S(2)}, u32[]{:S(2)}) collective-permute-start(bf16[2,256,512]{2,1,0:T(8,128)(2,1)} %get-tuple-element.62), channel_id=1, source_target_pairs={{0,24},{8,0},{16,8},{24,16},{1,25},{9,1},{17,9},{25,17},{2,26},{10... | collective-permute-start | bytes 1572872 | tf_op jit(solution)/shard_map/ppermute | solution.py:406
  31.6 0.0 copy-done.16
  31.6 0.0 copy-done.14
  31.6 2.5 %order.1 = (f32[1536,1]{1,0:T(8,128)}, f32[1536,1]{1,0:T(8,128)S(1)}) custom-call(s32[1,1536]{1,0:T(1,128)S(1)} %bitcast.14, s32[1,1536]{1,0:T(1,128)S(1)} %get-tuple-element.57.rank_ref), custom_call_target="tpu_custom_call" | custom-call | flops 18874368 | bytes 1 | tf_op jit(solution)/shard_map/order/pallas_call | solution.py:410
  34.1 6.8 %lookup.3 = bf16[8,128,512]{2,1,0:T(8,128)(2,1)S(1)} custom-call(s32[8,1,512]{2,1,0:T(1,128)S(1)} %all_to_all.19.ids_ref, bf16[4096,512]{1,0:T(8,128)(2,1)} %source_ref.3, f32[1536,1]{1,0:T(8,128)S(1)} %get-tuple-element.59._.slot_ref), custom_call_target="tpu_custom_call" | custom-call | flops 4294967296 | bytes 4194304 | tf_op jit(solution)/shard_map/lookup/pallas_call | solution.py:161
  41.0 0.0 copy-start.1
  41.0 1.0 copy-done.1
  42.0 0.9 copy-done.8
  42.9 7.6 %all-to-all-done.2 = bf16[8,112,512]{2,1,0:T(8,128)(2,1)S(1)} async-done(((bf16[8,112,512]{2,1,0:T(8,128)(2,1)}), bf16[8,112,512]{2,1,0:T(8,128)(2,1)S(1)}, u32[]{:S(2)}, u32[]{:S(2)}) %all-to-all-start.2) | async-done | bytes 917536 | tf_op jit(solution)/shard_map/all_to_all | solution.py:402
  50.5 0.9 copy-done.2
  51.4 3.7 %all-to-all-start.3 = ((bf16[8,128,512]{2,1,0:T(8,128)(2,1)}), bf16[8,128,512]{2,1,0:T(8,128)(2,1)S(1)}, u32[]{:S(2)}, u32[]{:S(2)}) async-start(bf16[8,128,512]{2,1,0:T(8,128)(2,1)} %copy-done.1), calls=%async_computation.3 | async-start | bytes 2097152 | tf_op jit(solution)/shard_map/all_to_all | solution.py:402
  55.2 0.6 compare_reduce_fusion
  56.5 0.0 copy-start.3
  56.5 0.0 collective-permute-done.refs_0_
  56.5 0.0 collective-permute-done.1.refs_1_
  56.5 0.0 collective-permute-done.2.refs_2_
  56.5 0.0 copy-done
  56.5 0.0 copy-done.5
  56.5 0.0 copy-done.7
  56.5 0.0 copy-start.6
  56.6 1.6 %copy-done.6 = bf16[2,512,1024]{2,1,0:T(8,128)(2,1)S(1)} copy-done((bf16[2,512,1024]{2,1,0:T(8,128)(2,1)S(1)}, bf16[2,512,1024]{2,1,0:T(8,128)(2,1)}, u32[]{:S(2)}) %copy-start.6) | copy-done | bytes 2097176
  58.2 0.0 copy-start.24
  58.2 5.1 %project.1 = (bf16[2,1024,512]{2,1,0:T(8,128)(2,1)S(1)}, bf16[2,1024,512]{2,1,0:T(8,128)(2,1)S(1)}) custom-call(s32[1,4]{1,0:T(1,128)S(1)} %copy-done.5, s32[1,4]{1,0:T(1,128)S(1)} %copy-done.7, bf16[2,4,256,512]{3,2,1,0:T(8,128)(2,1)S(1)} %copy-done, bf16[2,256,512]{2,1,0:T(8,128)(2,1)} %collective-permute-done.refs_0_, ...), custom_call_target="tpu_custom_call" | custom-call | flops 2147483648 | bytes 4194304 | tf_op jit(solution)/shard_map/project/pallas_call | solution.py:249
  63.3 0.0 copy-start.26
  63.3 0.0 copy-start.27
  63.3 0.0 copy-done.3
  63.3 0.0 copy-done.9
  63.4 20.9 %run_layers.4.source_ref = bf16[1152,512]{1,0:T(8,128)(2,1)S(1)} custom-call(f32[1536,1]{1,0:T(8,128)S(1)} %copy-done.9, bf16[896,512]{1,0:T(8,128)(2,1)S(1)} %bitcast.7, bf16[2,1024,512]{2,1,0:T(8,128)(2,1)S(1)} %get-tuple-element.63.refs_1_.refs_2_, bf16[2,1024,512]{2,1,0:T(8,128)(2,1)S(1)} %get-tuple-element.64.refs_2_.refs_3_, f32[2,512]{1,0:T(2,128)S(1)} %copy-done.19, ...), custom_call_target="tpu_custom_call" | custom-call | flops 13287555072 | bytes 8388608 | tf_op jit(solution)/shard_map/run_layers/pallas_call | solution.py:336
  84.3 0.0 copy-done.26
  84.3 0.0 copy-done.27
  84.3 0.0 copy-done.13
  84.3 0.0 copy-start.4
  84.3 0.0 copy-start.10
  84.3 3.7 %pick.3.refs_8_ = bf16[1536,512]{1,0:T(8,128)(2,1)} custom-call(f32[1536,1]{1,0:T(8,128)S(1)} %copy-done.13, bf16[1152,512]{1,0:T(8,128)(2,1)S(1)} %run_layers.4.source_ref), custom_call_target="tpu_custom_call" | custom-call | flops 1811939328 | bytes 1179648 | tf_op jit(solution)/shard_map/pick/pallas_call | solution.py:205
  88.0 0.0 all-to-all-done.3
  88.0 0.0 copy-start.12
  88.0 9.7 %run_layers.5 = bf16[384,512]{1,0:T(8,128)(2,1)S(1)} custom-call(f32[1536,1]{1,0:T(8,128)S(1)} %copy-done.10, bf16[896,512]{1,0:T(8,128)(2,1)S(1)} %bitcast.8, bf16[1024,512]{1,0:T(8,128)(2,1)S(1)} %bitcast.6, bf16[2,1024,512]{2,1,0:T(8,128)(2,1)} %copy-done.26, bf16[2,1024,512]{2,1,0:T(8,128)(2,1)} %copy-done.27, f32[2,512]{1,0:T(2,128)} %refs_4_.5, ...), custom_call_target="tpu_custom_call" | custom-call | flops 4429185024 | bytes 8388608 | tf_op jit(solution)/shard_map/run_layers/pallas_call | solution.py:336
  97.8 0.0 copy-done.12
  97.8 2.8 %conditional.1 = (bf16[1536,512]{1,0:T(8,128)(2,1)}) conditional(s32[]{:T(128)} %convert_element_type.3, (f32[1536,1]{1,0:T(8,128)S(1)}, bf16[384,512]{1,0:T(8,128)(2,1)S(1)}, bf16[1536,512]{1,0:T(8,128)(2,1)S(1)}) %tuple.18, (s32[8,1,512]{2,1,0:T(1,128)S(1)}, bf16[4096,512]{1,0:T(8,128)(2,1)}, s32[1,1536]{1,0:T(1,128)}, s32[1,1536]{1,0:T(1,128)}, ...), branch_computations={%region_1.0_spmd, %region_2.3_spmd} | conditional | flops 17716748288 | bytes 44228816 | solution.py:445
  97.8 2.8 %pick.2 = bf16[1536,512]{1,0:T(8,128)(2,1)} custom-call(f32[1536,1]{1,0:T(8,128)S(1)} %get-tuple-element.34.slot_ref, bf16[384,512]{1,0:T(8,128)(2,1)S(1)} %get-tuple-element.35.source_ref, bf16[1536,512]{1,0:T(8,128)(2,1)S(1)} %get-tuple-element.36.refs_0_), custom_call_target="tpu_custom_call" | custom-call | flops 603979776 | bytes 393216 | tf_op jit(solution)/shard_map/cond/branch_0_fun/pick/pallas_call | solution.py:205
  (19 shorter events, 0.0 us)
Async XLA Ops:
  0.0 17.9 %copy-start.18 = (f32[2,512]{1,0:T(2,128)S(1)}, f32[2,512]{1,0:T(2,128)}, u32[]{:S(2)}) copy-start(f32[2,512]{1,0:T(2,128)} %refs_4_.5) | copy-start | bytes 12292
  4.0 27.6 %copy-start.16 = (s32[1,1536]{1,0:T(1,128)}, s32[1,1536]{1,0:T(1,128)S(1)}, u32[]{:S(2)}) copy-start(s32[1,1536]{1,0:T(1,128)S(1)} %get-tuple-element.57.rank_ref) | copy-start | bytes 18436
  17.9 13.7 %copy-start.14 = (s32[1536,1]{0,1:T(1,128)S(1)}, s32[1536,1]{0,1:T(1,128)}, u32[]{:S(2)}) copy-start(s32[1536,1]{0,1:T(1,128)} %param.17) | copy-start | bytes 18436
  25.0 25.5 %all-to-all-start.2 = ((bf16[8,112,512]{2,1,0:T(8,128)(2,1)}), bf16[8,112,512]{2,1,0:T(8,128)(2,1)S(1)}, u32[]{:S(2)}, u32[]{:S(2)}) async-start(bf16[8,112,512]{2,1,0:T(8,128)(2,1)} %lookup.2), calls=%async_computation.2 | async-start | bytes 1835008 | tf_op jit(solution)/shard_map/all_to_all | solution.py:402
  28.6 27.9 %collective-permute-start = (bf16[2,256,512]{2,1,0:T(8,128)(2,1)}, bf16[2,256,512]{2,1,0:T(8,128)(2,1)}, u32[]{:S(2)}, u32[]{:S(2)}) collective-permute-start(bf16[2,256,512]{2,1,0:T(8,128)(2,1)} %get-tuple-element.60), channel_id=1, source_target_pairs={{0,8},{8,16},{16,24},{24,0},{1,9},{9,17},{17,25},{25,1},{2,10},{10... | collective-permute-start | bytes 1572872 | tf_op jit(solution)/shard_map/ppermute | solution.py:406
  28.6 27.8 %collective-permute-start.1 = (bf16[2,256,512]{2,1,0:T(8,128)(2,1)}, bf16[2,256,512]{2,1,0:T(8,128)(2,1)}, u32[]{:S(2)}, u32[]{:S(2)}) collective-permute-start(bf16[2,256,512]{2,1,0:T(8,128)(2,1)} %get-tuple-element.61), channel_id=1, source_target_pairs={{0,16},{8,24},{16,0},{24,8},{1,17},{9,25},{17,1},{25,9},{2,18},{10... | collective-permute-start | bytes 1572872 | tf_op jit(solution)/shard_map/ppermute | solution.py:406
  30.2 26.3 %collective-permute-start.2 = (bf16[2,256,512]{2,1,0:T(8,128)(2,1)}, bf16[2,256,512]{2,1,0:T(8,128)(2,1)}, u32[]{:S(2)}, u32[]{:S(2)}) collective-permute-start(bf16[2,256,512]{2,1,0:T(8,128)(2,1)} %get-tuple-element.62), channel_id=1, source_target_pairs={{0,24},{8,0},{16,8},{24,16},{1,25},{9,1},{17,9},{25,17},{2,26},{10... | collective-permute-start | bytes 1572872 | tf_op jit(solution)/shard_map/ppermute | solution.py:406
  41.0 1.0 copy-start.1
  42.0 0.9 copy-start.8
  42.9 13.7 %copy-start = (bf16[2,4,256,512]{3,2,1,0:T(8,128)(2,1)S(1)}, bf16[2,4,256,512]{3,2,1,0:T(8,128)(2,1)}, u32[]{:S(2)}) copy-start(bf16[2,4,256,512]{3,2,1,0:T(8,128)(2,1)} %history_ref.3) | copy-start | bytes 6291460
  42.9 13.7 %copy-start.5 = (s32[1,4]{1,0:T(1,128)S(1)}, s32[1,4]{1,0:T(1,128)}, u32[]{:S(2)}) copy-start(s32[1,4]{1,0:T(1,128)} %assignment_ref.3) | copy-start | bytes 52
  42.9 13.7 %copy-start.7 = (s32[1,4]{1,0:T(1,128)S(1)}, s32[1,4]{1,0:T(1,128)}, u32[]{:S(2)}) copy-start(s32[1,4]{1,0:T(1,128)} %lengths_ref.1) | copy-start | bytes 52
  50.5 0.9 copy-start.2
  51.4 36.6 %all-to-all-start.3 = ((bf16[8,128,512]{2,1,0:T(8,128)(2,1)}), bf16[8,128,512]{2,1,0:T(8,128)(2,1)S(1)}, u32[]{:S(2)}, u32[]{:S(2)}) async-start(bf16[8,128,512]{2,1,0:T(8,128)(2,1)} %copy-done.1), calls=%async_computation.3 | async-start | bytes 2097152 | tf_op jit(solution)/shard_map/all_to_all | solution.py:402
  56.5 6.8 %copy-start.3 = (bf16[8,112,512]{2,1,0:T(8,128)(2,1)S(1)}, bf16[8,112,512]{2,1,0:T(8,128)(2,1)}, u32[]{:S(2)}) copy-start(bf16[8,112,512]{2,1,0:T(8,128)(2,1)} %copy-done.2) | copy-start | bytes 2752516
  56.5 1.7 %copy-start.6 = (bf16[2,512,1024]{2,1,0:T(8,128)(2,1)S(1)}, bf16[2,512,1024]{2,1,0:T(8,128)(2,1)}, u32[]{:S(2)}) copy-start(bf16[2,512,1024]{2,1,0:T(8,128)(2,1)} %refs_4_.3) | copy-start | bytes 6291460
  58.2 5.1 %copy-start.9 = (f32[1536,1]{1,0:T(8,128)S(1)}, f32[1536,1]{1,0:T(8,128)}, u32[]{:S(2)}) copy-start(f32[1536,1]{1,0:T(8,128)} %copy-done.8) | copy-start | bytes 18436
  58.2 5.1 %copy-start.19 = (f32[2,512]{1,0:T(2,128)S(1)}, f32[2,512]{1,0:T(2,128)}, u32[]{:S(2)}) copy-start(f32[2,512]{1,0:T(2,128)} %refs_4_.5) | copy-start | bytes 12292
  58.2 5.1 %copy-start.21 = (bf16[2,512,1024]{2,1,0:T(8,128)(2,1)S(1)}, bf16[2,512,1024]{2,1,0:T(8,128)(2,1)}, u32[]{:S(2)}) copy-start(bf16[2,512,1024]{2,1,0:T(8,128)(2,1)} %refs_5_.3) | copy-start | bytes 6291460
  58.2 5.1 %copy-start.22 = (bf16[2,512,512]{2,1,0:T(8,128)(2,1)S(1)}, bf16[2,512,512]{2,1,0:T(8,128)(2,1)}, u32[]{:S(2)}) copy-start(bf16[2,512,512]{2,1,0:T(8,128)(2,1)} %refs_7_.1) | copy-start | bytes 3145732
  58.2 5.2 %copy-start.24 = (f32[2,512]{1,0:T(2,128)S(1)}, f32[2,512]{1,0:T(2,128)}, u32[]{:S(2)}) copy-start(f32[2,512]{1,0:T(2,128)} %refs_6_.3) | copy-start | bytes 12292
  63.3 21.0 %copy-start.26 = (bf16[2,1024,512]{2,1,0:T(8,128)(2,1)}, bf16[2,1024,512]{2,1,0:T(8,128)(2,1)S(1)}, u32[]{:S(2)}) copy-start(bf16[2,1024,512]{2,1,0:T(8,128)(2,1)S(1)} %get-tuple-element.63.refs_1_.refs_2_) | copy-start | bytes 6291460
  63.3 21.0 %copy-start.27 = (bf16[2,1024,512]{2,1,0:T(8,128)(2,1)}, bf16[2,1024,512]{2,1,0:T(8,128)(2,1)S(1)}, u32[]{:S(2)}) copy-start(bf16[2,1024,512]{2,1,0:T(8,128)(2,1)S(1)} %get-tuple-element.64.refs_2_.refs_3_) | copy-start | bytes 6291460
  63.4 20.9 %copy-start.13 = (f32[1536,1]{1,0:T(8,128)S(1)}, f32[1536,1]{1,0:T(8,128)}, u32[]{:S(2)}) copy-start(f32[1536,1]{1,0:T(8,128)} %get-tuple-element.58.slot_ref) | copy-start | bytes 18436
  84.3 3.7 %copy-start.4 = (bf16[8,112,512]{2,1,0:T(8,128)(2,1)S(1)}, bf16[8,112,512]{2,1,0:T(8,128)(2,1)}, u32[]{:S(2)}) copy-start(bf16[8,112,512]{2,1,0:T(8,128)(2,1)} %copy-done.2) | copy-start | bytes 2752516
  84.3 3.7 %copy-start.10 = (f32[1536,1]{1,0:T(8,128)S(1)}, f32[1536,1]{1,0:T(8,128)}, u32[]{:S(2)}) copy-start(f32[1536,1]{1,0:T(8,128)} %copy-done.8) | copy-start | bytes 18436
  88.0 9.7 %copy-start.12 = (bf16[1536,512]{1,0:T(8,128)(2,1)S(1)}, bf16[1536,512]{1,0:T(8,128)(2,1)}, u32[]{:S(2)}) copy-start(bf16[1536,512]{1,0:T(8,128)(2,1)} %pick.3.refs_8_) | copy-start | bytes 4718596
